TPU v7x, 32 devices: a whole 2x2x4 slice. The times are simulated.
32 devices in a mesh: mem: 8 (over z, x), geo: 4 (over y, core).
Axes of the slice: x: 2, y: 2, z: 4, core: 2. Of those that a mesh axis runs over, the one named last changes fastest.
Arguments:
- control: float32 [8, 32, 48, 384], P('mem', 'geo'), may hold values from -6 to 6
- kappa_table: float32 [16], replicated, may hold values from 0.02 to 0.24
- kappa_index: int32 [48, 384], replicated, may hold values from 0 to 15
- tile_bounds: int32 [5], replicated, may hold values from 0 to 18432, as said below
- filter_bands: float32 [4, 5, 32], replicated, may hold values from -0.3 to 0.3
- perturbation: bfloat16 [2, 8, 32, 18432], P(None, 'mem', None, 'geo'), may hold values from -6 to 6
Outputs:
- increment: float32 [2, 32, 18432], P(None, 'mem', 'geo')
Inputs may be any that keep to these rules, and one draw needn't show every extreme that they name: tile_bounds[0] is 0, tile_bounds[4] is 18432, and the bounds never fall; tile t holds columns tile_bounds[t] to tile_bounds[t + 1] - 1.
All inputs are finite; a program needn't handle non-finite values.
Results may differ from a plain program's by a relative error of at most 0.005.
Values may be sent and summed in bfloat16 or wider, within the bound.
A program may use at most 64 MiB of HBM per device.

v0:
```python
import jax
import jax.numpy as jnp
from jax import lax
from jax.sharding import PartitionSpec as P

ITERS = 10


def neighbours(state):
    east = jnp.concatenate([state[..., 1:, :], state[..., -1:, :]], axis=-2)
    west = jnp.concatenate([state[..., :1, :], state[..., :-1, :]], axis=-2)
    north = jnp.concatenate([state[..., 1:], state[..., -1:]], axis=-1)
    south = jnp.concatenate([state[..., :1], state[..., :-1]], axis=-1)
    return (east, west, north, south)


def face_weights(kappa_field):
    return tuple((0.5 * (kappa_field + other) for other in neighbours(kappa_field)))


def diffuse_step(state, weights):
    east, west, north, south = neighbours(state)
    update = weights[0] * (east - state) + weights[1] * (west - state)
    update = update + weights[2] * (north - state) + weights[3] * (south - state)
    return state + update


def vertical_filter(values, coefficients):
    levels = values.shape[0]
    padded = jnp.pad(values, ((2, 2), (0, 0)))
    result = values
    for offset in range(5):
        result = result + coefficients[offset] * padded[offset : offset + levels]
    return result


def body(control, kappa_table, kappa_index, tile_bounds, filter_bands, perturbation):
    moved_pert = lax.all_to_all(perturbation, "mem", split_axis=2, concat_axis=1, tiled=True)
    kappa_field = jnp.zeros(kappa_index.shape, jnp.float32)
    for entry in range(kappa_table.shape[0]):
        kappa_field = kappa_field + jnp.where(kappa_index == entry, kappa_table[entry], 0.0)
    weights = face_weights(kappa_field)
    state_field = lax.fori_loop(0, ITERS, lambda step, cur: diffuse_step(cur, weights), control)
    flattened = state_field.reshape(state_field.shape[0], state_field.shape[1], -1)
    by_columns = lax.all_to_all(flattened, "geo", split_axis=2, concat_axis=1, tiled=True)
    width = by_columns.shape[2]
    tiles_count = filter_bands.shape[0]
    columns = lax.axis_index("geo") * width + jnp.arange(width, dtype=jnp.int32)
    tile_ids = jnp.sum((columns[None, :] >= tile_bounds[1:-1][:, None]).astype(jnp.int32), axis=0)
    one_hot = (tile_ids[None, :] == jnp.arange(tiles_count, dtype=jnp.int32)[:, None]).astype(
        jnp.float32
    )
    coefficients = jnp.einsum("tkl,tc->klc", filter_bands, one_hot, precision=lax.Precision.HIGHEST)
    filtered = vertical_filter(by_columns[0], coefficients).astype(jnp.bfloat16)
    moved_filtered = lax.all_to_all(filtered[None], "mem", split_axis=1, concat_axis=0, tiled=True)
    return jnp.sum(
        moved_pert.astype(jnp.float32) * moved_filtered.astype(jnp.float32)[None], axis=1
    )


def solution(mesh):
    in_specs = (P("mem", "geo", None, None), P(), P(), P(), P(), P(None, "mem", None, "geo"))
    out_specs = P(None, "mem", "geo")
    return jax.shard_map(body, mesh=mesh, in_specs=in_specs, out_specs=out_specs, check_vma=False)
```

profile of v0, /device:TPU:0, one launch (start us, length us, event | category | flops | bytes accessed | tf_op | source)
XLA Modules:
  0.0 219.2 jit_solution(1623861114880907975)
XLA Ops:
  0.0 1.1 copy.36
  1.1 1.9 fusion.36
  3.0 10.8 %select_add_fusion = f32[48,384]{1,0:T(8,128)S(1)} fusion(s32[48,384]{1,0:T(8,128)} %param.10, f32[]{:T(128)} %bitcast.16, f32[]{:T(128)} %bitcast.15, f32[]{:T(128)} %bitcast.14, f32[]{:T(128)} %bitcast.13, f32[]{:T(128)} %bitcast.12, f32[]{:T(128)} %bitcast.11, f32[]{:T(128)} %bitcast.10, f32[]{:T(128)} %bitcast.9, f32[]{:T(128)} %bitcast.8, f32[]{:T(128)} %bitcast.7, ...), kind=kLoop, calls=%fused_computation.47 | loop fusion | flops 866304 | bytes 147520 | tf_op jit(solution)/shard_map/add | solution.py:41
  14.1 10.9 %fusion.24 = (f32[48,384]{1,0:T(8,128)S(1)}, f32[48,384]{1,0:T(8,128)S(1)}, f32[48,384]{1,0:T(8,128)S(1)}, f32[48,384]{1,0:T(8,128)S(1)}) fusion(f32[48,383]{1,0:T(8,128)S(1)} %get-tuple-element.64, f32[48,1]{1,0:T(8,128)S(1)} %get-tuple-element.62, f32[48,1]{1,0:T(8,128)S(1)} %get-tuple-element.63, f32[48,383]{1,0:T(8,128)S(1)} %get-tuple-element.65, ...), kind=kLoop, calls=%fused_computation.44 | loop fusion | flops 1087488 | bytes 663616 | tf_op jit(solution)/shard_map/mul | solution.py:18
  24.9 10.2 %while.10 = (s32[]{:T(128)}, f32[1,8,48,384]{3,2,1,0:T(8,128)S(1)}, f32[48,384]{1,0:T(8,128)S(1)}, f32[48,384]{1,0:T(8,128)S(1)}, f32[48,384]{1,0:T(8,128)S(1)}, /*index=5*/f32[48,384]{1,0:T(8,128)S(1)}, s32[]{:T(128)}) while((s32[]{:T(128)}, f32[1,8,48,384]{3,2,1,0:T(8,128)S(1)}, f32[48,384]{1,0:T(8,128)S(1)}, f32[48,384]{1,0:T(8,128)S(1)}, ...), condition=%wide.region_1.2_spmd, body=%wide.region_0.1_spmd.sunk | while | flops 2359298 | bytes 8552525 | solution.py:43
  35.2 5.5 %copy.21 = f32[1,8,48,384]{1,3,2,0:T(8,128)} copy(f32[1,8,48,384]{3,2,1,0:T(8,128)S(1)} %get-tuple-element.37) | data formatting | bytes 1179648 | tf_op jit(solution)/shard_map/while | solution.py:43
  41.2 83.6 %reduce.2 = f32[18432,8]{1,0:T(8,128)} reduce(f32[18432,1,8]{2,1,0:T(1,128)} %bitcast.70, f32[]{:T(128)} %broadcast.28), dimensions={1}, to_apply=%bitcast.62.reduce_sub_computation | reduce | bytes 1179652
  124.8 7.8 %reshape.43 = f32[4,1,36864]{2,1,0:T(1,128)} reshape(f32[18432,8]{1,0:T(8,128)} %reduce.2) | data formatting | bytes 1179648
  132.6 4.3 %all-to-all-start.1 = ((f32[4,1,36864]{2,1,0:T(1,128)}), f32[4,1,36864]{2,1,0:T(1,128)}, u32[]{:S(2)}, u32[]{:S(2)}) async-start(f32[4,1,36864]{2,1,0:T(1,128)} %reshape.43), calls=%async_computation.1 | async-start | bytes 1179648 | tf_op jit(solution)/shard_map/all_to_all | solution.py:45
  137.2 1.3 convolution_bitcast_fusion
  138.5 8.5 %all-to-all-done.1 = f32[4,1,36864]{2,1,0:T(1,128)} async-done(((f32[4,1,36864]{2,1,0:T(1,128)}), f32[4,1,36864]{2,1,0:T(1,128)}, u32[]{:S(2)}, u32[]{:S(2)}) %all-to-all-start.1) | async-done | bytes 589856 | tf_op jit(solution)/shard_map/all_to_all | solution.py:45
  147.0 3.3 %reduce.3 = f32[4,36864]{1,0:T(4,128)S(1)} reduce(f32[4,1,36864]{2,1,0:T(1,128)} %all-to-all-done.1, f32[]{:T(128)} %broadcast.28), dimensions={1}, to_apply=%all_to_all.11.reduce_sub_computation | reduce | bytes 1179652 | tf_op jit(solution)/shard_map/all_to_all | solution.py:45
  150.3 22.3 %reshape.44 = f32[18432,1,8]{2,1,0:T(1,128)} reshape(f32[4,36864]{1,0:T(4,128)S(1)} %reduce.3) | data formatting | bytes 1179648
  172.6 5.5 %copy.22 = f32[1,8,4,4608]{3,1,2,0:T(8,128)S(1)} copy(f32[1,8,4,4608]{1,3,2,0:T(8,128)} %bitcast.71) | data formatting | bytes 1179648 | tf_op jit(solution)/shard_map/all_to_all | solution.py:45
  179.5 2.5 %reduce.4 = bf16[32,4608]{1,0:T(8,128)(2,1)S(1)} reduce(bf16[32,1,4608]{2,1,0:T(2,128)(2,1)S(1)} %bitcast.72, bf16[]{:T(256)} %broadcast.30), dimensions={1}, to_apply=%bitcast.69.reduce_sub_computation | reduce | bytes 589826
  181.9 0.9 reshape.45
  182.8 6.6 %all-to-all-start.2 = ((bf16[8,2,9216]{2,1,0:T(2,128)(2,1)}), bf16[8,2,9216]{2,1,0:T(2,128)(2,1)S(1)}, u32[]{:S(2)}, u32[]{:S(2)}) async-start(bf16[8,2,9216]{2,1,0:T(2,128)(2,1)} %reshape.45), calls=%async_computation.2 | async-start | bytes 589824 | tf_op jit(solution)/shard_map/all_to_all | solution.py:55
  189.4 1.4 copy.20
  190.8 7.9 %all-to-all-done.2 = bf16[8,2,9216]{2,1,0:T(2,128)(2,1)S(1)} async-done(((bf16[8,2,9216]{2,1,0:T(2,128)(2,1)}), bf16[8,2,9216]{2,1,0:T(2,128)(2,1)S(1)}, u32[]{:S(2)}, u32[]{:S(2)}) %all-to-all-start.2) | async-done | bytes 294944 | tf_op jit(solution)/shard_map/all_to_all | solution.py:55
  198.7 3.6 %all-to-all-start = ((bf16[2,1,32,4608]{3,0,1,2:T(2,128)(2,1)}), bf16[2,1,32,4608]{3,0,1,2:T(2,128)(2,1)S(1)}, u32[]{:S(2)}, u32[]{:S(2)}) async-start(bf16[2,1,32,4608]{3,0,1,2:T(2,128)(2,1)} %copy.20), calls=%async_computation | async-start | bytes 1179648 | tf_op jit(solution)/shard_map/all_to_all | solution.py:38
  202.6 1.7 convert_reduce_fusion
  204.5 13.4 %all-to-all-done = bf16[2,1,32,4608]{3,0,1,2:T(2,128)(2,1)S(1)} async-done(((bf16[2,1,32,4608]{3,0,1,2:T(2,128)(2,1)}), bf16[2,1,32,4608]{3,0,1,2:T(2,128)(2,1)S(1)}, u32[]{:S(2)}, u32[]{:S(2)}) %all-to-all-start) | async-done | bytes 589856 | tf_op jit(solution)/shard_map/all_to_all | solution.py:38
  217.9 0.6 fusion.8
  218.5 0.7 copy.24
  (69 shorter events, 12.4 us)
Async XLA Ops:
  0.0 137.2 %copy-start = (f32[4,5,32]{2,0,1:T(4,128)S(1)}, f32[4,5,32]{2,0,1:T(4,128)}, u32[]{:S(2)}) copy-start(f32[4,5,32]{2,0,1:T(4,128)} %param.12) | copy-start | bytes 7684
  124.8 12.2 %copy-start.2 = (s32[5]{0:T(128)S(1)}, s32[5]{0:T(128)}, u32[]{:S(2)}) copy-start(s32[5]{0:T(128)} %param.11) | copy-start | bytes 64
  132.6 14.4 %all-to-all-start.1 = ((f32[4,1,36864]{2,1,0:T(1,128)}), f32[4,1,36864]{2,1,0:T(1,128)}, u32[]{:S(2)}, u32[]{:S(2)}) async-start(f32[4,1,36864]{2,1,0:T(1,128)} %reshape.43), calls=%async_computation.1 | async-start | bytes 1179648 | tf_op jit(solution)/shard_map/all_to_all | solution.py:45
  178.5 10.9 %copy-start.1 = (bf16[2,1,32,4608]{3,2,1,0:T(8,128)(2,1)S(1)}, bf16[2,1,32,4608]{3,2,1,0:T(8,128)(2,1)}, u32[]{:S(2)}) copy-start(bf16[2,1,32,4608]{3,2,1,0:T(8,128)(2,1)} %param.13) | copy-start | bytes 1769476
  182.8 15.8 %all-to-all-start.2 = ((bf16[8,2,9216]{2,1,0:T(2,128)(2,1)}), bf16[8,2,9216]{2,1,0:T(2,128)(2,1)S(1)}, u32[]{:S(2)}, u32[]{:S(2)}) async-start(bf16[8,2,9216]{2,1,0:T(2,128)(2,1)} %reshape.45), calls=%async_computation.2 | async-start | bytes 589824 | tf_op jit(solution)/shard_map/all_to_all | solution.py:55
  198.7 19.2 %all-to-all-start = ((bf16[2,1,32,4608]{3,0,1,2:T(2,128)(2,1)}), bf16[2,1,32,4608]{3,0,1,2:T(2,128)(2,1)S(1)}, u32[]{:S(2)}, u32[]{:S(2)}) async-start(bf16[2,1,32,4608]{3,0,1,2:T(2,128)(2,1)} %copy.20), calls=%async_computation | async-start | bytes 1179648 | tf_op jit(solution)/shard_map/all_to_all | solution.py:38
where the time goes:
time: 220 us; the launch traced here: 219 us
  other arithmetic  119 us (54%)
  local copies, waits for them, and re-layouts  53.6 us (24%)
  waiting for transfers between devices  29.8 us (14%)
  starting transfers between devices  14.5 us (7%)
    unnamed x2, other arithmetic  86 us
    unnamed x14, local copies, waits for them, and re-layouts  34.8 us
    all_to_all x1, waiting for transfers between devices, body(): lax.all_to_all(perturbation, 'mem', split_axis=2, concat_axis=1, tiled=True)  13.4 us
    mul x1, other arithmetic, face_weights(): 0.5 * (kappa_field + other)  10.9 us
    add x1, other arithmetic, body(): kappa_field + jnp.where(kappa_index == entry, kappa_table[entry], 0.0)  10.8 us
    all_to_all x1, waiting for transfers between devices, body(): lax.all_to_all(flattened, 'geo', split_axis=2, concat_axis=1, tiled=True)  8.52 us
    all_to_all x1, waiting for transfers between devices, body(): lax.all_to_all(filtered[None], 'mem', split_axis=1, concat_axis=0, tiled=...  7.85 us
    all_to_all x1, starting transfers between devices, body(): lax.all_to_all(filtered[None], 'mem', split_axis=1, concat_axis=0, tiled=...  6.57 us
  transfers between devices with their start and end apart: 3, of which 3 were waited for; matrix products, arithmetic and copies ran while one was open for 2% of the time, Pallas kernels for 0%

commit v1 on v0

--- a/solution.py
+++ b/solution.py
@@ -4,6 +4,30 @@
 from jax.sharding import PartitionSpec as P
 
 ITERS = 10
+
+
+def in_blocks(array, dim, size):
+    lengths = array.shape
+    tiles = array.reshape(*lengths[:dim], size, lengths[dim] // size, *lengths[dim + 1 :])
+    return jnp.moveaxis(tiles, dim, 0)
+
+
+def joined_along(blocks, dim):
+    lengths = list(blocks.shape[1:])
+    lengths[dim] *= blocks.shape[0]
+    return jnp.moveaxis(blocks, 0, dim).reshape(lengths)
+
+
+def rotated_exchange(array, axis, split_dim, concat_dim):
+    size, here = (lax.axis_size(axis), lax.axis_index(axis))
+    tiles = in_blocks(array, split_dim, size)
+    out = tiles
+    for step in range(1, size):
+        target, source = ((here + step) % size, (here - step) % size)
+        sent = lax.dynamic_index_in_dim(tiles, target, 0)
+        partner_block = lax.ppermute(sent, axis, [(i, (i + step) % size) for i in range(size)])
+        out = lax.dynamic_update_slice_in_dim(out, partner_block, source, axis=0)
+    return joined_along(out, concat_dim)
 
 
 def neighbours(state):
@@ -42,7 +66,7 @@
     weights = face_weights(kappa_field)
     state_field = lax.fori_loop(0, ITERS, lambda step, cur: diffuse_step(cur, weights), control)
     flattened = state_field.reshape(state_field.shape[0], state_field.shape[1], -1)
-    by_columns = lax.all_to_all(flattened, "geo", split_axis=2, concat_axis=1, tiled=True)
+    by_columns = rotated_exchange(flattened, "geo", 2, 1)
     width = by_columns.shape[2]
     tiles_count = filter_bands.shape[0]
     columns = lax.axis_index("geo") * width + jnp.arange(width, dtype=jnp.int32)

time: 220 us -> 93.5 us (0.42)
  other arithmetic: 119 us -> 35.2 us
  local copies, waits for them, and re-layouts: 53.6 us -> 20.3 us
  waiting for transfers between devices: 29.8 us -> 21.5 us
    unnamed x2 -> x1, other arithmetic: 86 us -> 2.47 us
    unnamed x14, local copies, waits for them, and re-layouts: 34.8 us -> 6.18 us
    all_to_all x1 -> x0, waiting for transfers between devices: 8.52 us -> none  [body(): lax.all_to_all(flattened, 'geo', split_axis=2, concat_axis=1, tiled=True)]
    while x1 -> x0, local copies, waits for them, and re-layouts: 5.53 us -> none  [body(): lax.fori_loop(0, ITERS, lambda step, cur: diffuse_step(cur, weights), con...]
    all_to_all x1 -> x0, local copies, waits for them, and re-layouts: 5.48 us -> none  [body(): lax.all_to_all(flattened, 'geo', split_axis=2, concat_axis=1, tiled=True)]
    dynamic_update_slice x0 -> x3, local copies, waits for them, and re-layouts: none -> 4.73 us  [rotated_exchange(): out = lax.dynamic_update_slice_in_dim(out, partner_block, source, axis=0)]
    ppermute x0 -> x3, starting transfers between devices: none -> 4.46 us  [rotated_exchange(): lax.ppermute(sent, axis, [(i, (i + step) % size) for i in range(size)])]
    all_to_all x1 -> x0, starting transfers between devices: 4.32 us -> none  [body(): lax.all_to_all(flattened, 'geo', split_axis=2, concat_axis=1, tiled=True)]
  transfers between devices with their start and end apart: 3 -> 5, of which waited for: 3 -> 2; matrix products, arithmetic and copies ran while one was open for 2% -> 11% of each run, Pallas kernels for 0% -> 0%
where the time goes in v1:
time: 93.5 us; the launch traced here: 92.7 us
  other arithmetic  35.2 us (38%)
  waiting for transfers between devices  21.5 us (23%)
  local copies, waits for them, and re-layouts  20.3 us (22%)
  starting transfers between devices  13.9 us (15%)
  matrix products  1.34 us (1%)
    all_to_all x1, waiting for transfers between devices, body(): lax.all_to_all(perturbation, 'mem', split_axis=2, concat_axis=1, tiled=True)  13.4 us
    mul x1, other arithmetic, face_weights(): 0.5 * (kappa_field + other)  11 us
    add x1, other arithmetic, body(): kappa_field + jnp.where(kappa_index == entry, kappa_table[entry], 0.0)  11 us
    all_to_all x1, waiting for transfers between devices, body(): lax.all_to_all(filtered[None], 'mem', split_axis=1, concat_axis=0, tiled=...  8.07 us
    unnamed x14, local copies, waits for them, and re-layouts  6.18 us
    all_to_all x1, starting transfers between devices, body(): lax.all_to_all(filtered[None], 'mem', split_axis=1, concat_axis=0, tiled=...  5.81 us
    add x10, other arithmetic, diffuse_step(): return state + update  5.51 us
    dynamic_update_slice x3, local copies, waits for them, and re-layouts, rotated_exchange(): out = lax.dynamic_update_slice_in_dim(out, partner_block, source, axis=0)  4.73 us
  transfers between devices with their start and end apart: 5, of which 2 were waited for; matrix products, arithmetic and copies ran while one was open for 11% of the time, Pallas kernels for 0%

profile of v1, /device:TPU:0, one launch (start us, length us, event | category | flops | bytes accessed | tf_op | source)
XLA Modules:
  0.0 92.7 jit_solution(1264410682293870148)
XLA Ops:
  0.0 1.1 %copy.46 = f32[1,8,48,384]{3,2,1,0:T(8,128)S(1)} copy(f32[1,8,48,384]{3,2,1,0:T(8,128)} %param.8) | data formatting | bytes 1179648
  1.1 2.0 %fusion.36 = (f32[1]{0:T(128)}, f32[1]{0:T(128)}, f32[1]{0:T(128)}, f32[1]{0:T(128)}, f32[1]{0:T(128)}, /*index=5*/f32[1]{0:T(128)}, f32[1]{0:T(128)}, f32[1]{0:...) fusion(f32[16]{0:T(128)} %param.9), kind=kLoop, calls=%fused_computation.69 | loop fusion | bytes 128 | tf_op jit(solution)/shard_map/slice | solution.py:65
  3.0 11.0 %select_add_fusion = f32[48,384]{1,0:T(8,128)S(1)} fusion(s32[48,384]{1,0:T(8,128)} %param.10, f32[]{:T(128)} %bitcast.16, f32[]{:T(128)} %bitcast.15, f32[]{:T(128)} %bitcast.14, f32[]{:T(128)} %bitcast.13, f32[]{:T(128)} %bitcast.12, f32[]{:T(128)} %bitcast.11, f32[]{:T(128)} %bitcast.10, f32[]{:T(128)} %bitcast.9, f32[]{:T(128)} %bitcast.8, f32[]{:T(128)} %bitcast.7, ...), kind=kLoop, calls=%fused_computation.51 | loop fusion | flops 866304 | bytes 147520 | tf_op jit(solution)/shard_map/add | solution.py:65
  14.2 11.0 %fusion.24 = (f32[48,384]{1,0:T(8,128)S(1)}, f32[48,384]{1,0:T(8,128)S(1)}, f32[48,384]{1,0:T(8,128)S(1)}, f32[48,384]{1,0:T(8,128)S(1)}) fusion(f32[48,383]{1,0:T(8,128)S(1)} %get-tuple-element.67, f32[48,1]{1,0:T(8,128)S(1)} %get-tuple-element.65, f32[48,1]{1,0:T(8,128)S(1)} %get-tuple-element.66, f32[48,383]{1,0:T(8,128)S(1)} %get-tuple-element.68, ...), kind=kLoop, calls=%fused_computation.48 | loop fusion | flops 1087488 | bytes 663616 | tf_op jit(solution)/shard_map/mul | solution.py:42
  25.3 10.2 %while.10 = (s32[]{:T(128)}, f32[1,8,48,384]{3,2,1,0:T(8,128)S(1)}, f32[48,384]{1,0:T(8,128)S(1)}, f32[48,384]{1,0:T(8,128)S(1)}, f32[48,384]{1,0:T(8,128)S(1)}, /*index=5*/f32[48,384]{1,0:T(8,128)S(1)}, s32[]{:T(128)}) while((s32[]{:T(128)}, f32[1,8,48,384]{3,2,1,0:T(8,128)S(1)}, f32[48,384]{1,0:T(8,128)S(1)}, f32[48,384]{1,0:T(8,128)S(1)}, ...), condition=%wide.region_1.2_spmd, body=%wide.region_0.1_spmd.sunk | while | flops 2359298 | bytes 8552525 | solution.py:67
  36.1 0.7 copy.34
  37.9 2.5 %collective-permute-start.1 = (f32[1,1,8,4608]{3,2,0,1:T(8,128)}, f32[1,1,8,4608]{3,2,0,1:T(8,128)}, u32[]{:S(2)}, u32[]{:S(2)}) collective-permute-start(f32[1,1,8,4608]{3,2,0,1:T(8,128)} %bitcast.75), channel_id=1, source_target_pairs={{0,2},{1,3},{2,0},{3,1},{4,6},{5,7},{6,4},{7,5},{8,10},{9,11},{10,... | collective-permute-start | bytes 442376 | tf_op jit(solution)/shard_map/ppermute | solution.py:28
  40.5 0.7 copy.32
  41.1 1.5 %collective-permute-start.2 = (f32[1,1,8,4608]{3,2,0,1:T(8,128)}, f32[1,1,8,4608]{3,2,0,1:T(8,128)}, u32[]{:S(2)}, u32[]{:S(2)}) collective-permute-start(f32[1,1,8,4608]{3,2,0,1:T(8,128)} %bitcast.74), channel_id=1, source_target_pairs={{0,3},{1,0},{2,1},{3,2},{4,7},{5,4},{6,5},{7,6},{8,11},{9,8},{10,9... | collective-permute-start | bytes 442376 | tf_op jit(solution)/shard_map/ppermute | solution.py:28
  42.8 1.3 %convolution_bitcast_fusion = f32[5,32,4608]{2,1,0:T(8,128)S(1)} fusion(f32[4,5,32]{2,0,1:T(4,128)S(1)} %copy-done, s32[4608]{0:T(1024)S(1)} %convert_reduce_fusion.1), kind=kOutput, calls=%fused_computation.12 | convolution fusion | flops 35407872 | bytes 2970112 | tf_op jit(solution)/shard_map/tkl,tc->klc/dot_general | solution.py:77
  44.2 1.0 %copy.31 = f32[1,8,4,4608]{3,1,2,0:T(8,128)} copy(f32[1,8,4,4608]{3,2,1,0:T(4,128)S(1)} %reshape_reshape.3) | data formatting | bytes 1179648 | tf_op jit(solution)/shard_map/reshape;reshape | solution.py:11
  45.2 1.6 %constant_dynamic-update-slice_fusion.2 = f32[4,1,8,4608]{3,2,0,1:T(8,128)} fusion(f32[4,1,8,4608]{3,2,0,1:T(8,128)} %bitcast.80, f32[1,1,8,4608]{3,2,0,1:T(8,128)} %collective-permute-done, s32[]{:T(128)S(6)} %select_n.114), kind=kLoop, calls=%fused_computation.59 | loop fusion | bytes 294916 | tf_op jit(solution)/shard_map/dynamic_update_slice | solution.py:29
  46.7 1.6 %constant_dynamic-update-slice_fusion.1 = f32[4,1,8,4608]{3,2,0,1:T(8,128)} fusion(f32[4,1,8,4608]{3,2,0,1:T(8,128)} %constant_dynamic-update-slice_fusion.2, f32[1,1,8,4608]{3,2,0,1:T(8,128)} %collective-permute-done.1, s32[]{:T(128)S(6)} %select_n.118), kind=kLoop, calls=%fused_computation.57 | loop fusion | bytes 294916 | tf_op jit(solution)/shard_map/dynamic_update_slice | solution.py:29
  48.3 1.6 %constant_dynamic-update-slice_fusion = f32[4,1,8,4608]{3,2,0,1:T(8,128)} fusion(f32[4,1,8,4608]{3,2,0,1:T(8,128)} %constant_dynamic-update-slice_fusion.1, f32[1,1,8,4608]{3,2,0,1:T(8,128)} %collective-permute-done.2, s32[]{:T(128)S(6)} %select_n.122), kind=kLoop, calls=%fused_computation.55 | loop fusion | bytes 294916 | tf_op jit(solution)/shard_map/dynamic_update_slice | solution.py:29
  49.9 2.7 %fusion.20 = bf16[1,32,4608]{2,1,0:T(8,128)(2,1)S(1)} fusion(f32[32,4608]{1,0:T(8,128)} %bitcast.81, f32[5,32,4608]{2,1,0:T(8,128)S(1)} %convolution_bitcast_fusion), kind=kLoop, calls=%fused_computation.37 | loop fusion | flops 1622016 | bytes 3833856 | tf_op jit(solution)/shard_map/broadcast_in_dim | solution.py:79
  53.6 2.5 %reduce.2 = bf16[32,4608]{1,0:T(8,128)(2,1)S(1)} reduce(bf16[32,1,4608]{2,1,0:T(2,128)(2,1)S(1)} %bitcast.78, bf16[]{:T(256)} %broadcast.34), dimensions={1}, to_apply=%bitcast.77.reduce_sub_computation | reduce | bytes 589826
  56.0 0.9 reshape.41
  57.0 5.8 %all-to-all-start.1 = ((bf16[8,2,9216]{2,1,0:T(2,128)(2,1)}), bf16[8,2,9216]{2,1,0:T(2,128)(2,1)S(1)}, u32[]{:S(2)}, u32[]{:S(2)}) async-start(bf16[8,2,9216]{2,1,0:T(2,128)(2,1)} %reshape.41), calls=%async_computation.1 | async-start | bytes 589824 | tf_op jit(solution)/shard_map/all_to_all | solution.py:79
  62.8 1.4 %copy.18 = bf16[2,1,32,4608]{3,0,1,2:T(2,128)(2,1)} copy(bf16[2,1,32,4608]{3,2,1,0:T(8,128)(2,1)S(1)} %copy-done.1) | data formatting | bytes 1179648 | tf_op args[5]
  64.2 8.1 %all-to-all-done.1 = bf16[8,2,9216]{2,1,0:T(2,128)(2,1)S(1)} async-done(((bf16[8,2,9216]{2,1,0:T(2,128)(2,1)}), bf16[8,2,9216]{2,1,0:T(2,128)(2,1)S(1)}, u32[]{:S(2)}, u32[]{:S(2)}) %all-to-all-start.1) | async-done | bytes 294944 | tf_op jit(solution)/shard_map/all_to_all | solution.py:79
  72.3 3.6 %all-to-all-start = ((bf16[2,1,32,4608]{3,0,1,2:T(2,128)(2,1)}), bf16[2,1,32,4608]{3,0,1,2:T(2,128)(2,1)S(1)}, u32[]{:S(2)}, u32[]{:S(2)}) async-start(bf16[2,1,32,4608]{3,0,1,2:T(2,128)(2,1)} %copy.18), calls=%async_computation | async-start | bytes 1179648 | tf_op jit(solution)/shard_map/all_to_all | solution.py:62
  76.1 1.7 %convert_reduce_fusion = f32[32,4608]{1,0:T(8,128)S(1)} fusion(bf16[32,1,4608]{2,1,0:T(2,128)(2,1)S(1)} %reshape.42), kind=kLoop, calls=%fused_computation.36 | loop fusion | flops 147456 | bytes 884736 | tf_op jit(solution)/shard_map/convert_element_type | solution.py:81
  78.0 13.4 %all-to-all-done = bf16[2,1,32,4608]{3,0,1,2:T(2,128)(2,1)S(1)} async-done(((bf16[2,1,32,4608]{3,0,1,2:T(2,128)(2,1)}), bf16[2,1,32,4608]{3,0,1,2:T(2,128)(2,1)S(1)}, u32[]{:S(2)}, u32[]{:S(2)}) %all-to-all-start) | async-done | bytes 589856 | tf_op jit(solution)/shard_map/all_to_all | solution.py:62
  92.0 0.7 copy.21
  (75 shorter events, 14.0 us)
Async XLA Ops:
  0.0 42.8 %copy-start = (f32[4,5,32]{2,0,1:T(4,128)S(1)}, f32[4,5,32]{2,0,1:T(4,128)}, u32[]{:S(2)}) copy-start(f32[4,5,32]{2,0,1:T(4,128)} %param.12) | copy-start | bytes 7684
  35.5 7.1 %copy-start.2 = (s32[5]{0:T(128)S(1)}, s32[5]{0:T(128)}, u32[]{:S(2)}) copy-start(s32[5]{0:T(128)} %param.11) | copy-start | bytes 64
  36.8 8.4 %collective-permute-start = (f32[1,1,8,4608]{3,2,0,1:T(8,128)}, f32[1,1,8,4608]{3,2,0,1:T(8,128)}, u32[]{:S(2)}, u32[]{:S(2)}) collective-permute-start(f32[1,1,8,4608]{3,2,0,1:T(8,128)} %bitcast.76), channel_id=1, source_target_pairs={{0,1},{1,2},{2,3},{3,0},{4,5},{5,6},{6,7},{7,4},{8,9},{9,10},{10,1... | collective-permute-start | bytes 442376 | tf_op jit(solution)/shard_map/ppermute | solution.py:28
  37.9 8.8 %collective-permute-start.1 = (f32[1,1,8,4608]{3,2,0,1:T(8,128)}, f32[1,1,8,4608]{3,2,0,1:T(8,128)}, u32[]{:S(2)}, u32[]{:S(2)}) collective-permute-start(f32[1,1,8,4608]{3,2,0,1:T(8,128)} %bitcast.75), channel_id=1, source_target_pairs={{0,2},{1,3},{2,0},{3,1},{4,6},{5,7},{6,4},{7,5},{8,10},{9,11},{10,... | collective-permute-start | bytes 442376 | tf_op jit(solution)/shard_map/ppermute | solution.py:28
  41.1 7.2 %collective-permute-start.2 = (f32[1,1,8,4608]{3,2,0,1:T(8,128)}, f32[1,1,8,4608]{3,2,0,1:T(8,128)}, u32[]{:S(2)}, u32[]{:S(2)}) collective-permute-start(f32[1,1,8,4608]{3,2,0,1:T(8,128)} %bitcast.74), channel_id=1, source_target_pairs={{0,3},{1,0},{2,1},{3,2},{4,7},{5,4},{6,5},{7,6},{8,11},{9,8},{10,9... | collective-permute-start | bytes 442376 | tf_op jit(solution)/shard_map/ppermute | solution.py:28
  49.9 12.9 %copy-start.1 = (bf16[2,1,32,4608]{3,2,1,0:T(8,128)(2,1)S(1)}, bf16[2,1,32,4608]{3,2,1,0:T(8,128)(2,1)}, u32[]{:S(2)}) copy-start(bf16[2,1,32,4608]{3,2,1,0:T(8,128)(2,1)} %param.13) | copy-start | bytes 1769476
  57.0 15.3 %all-to-all-start.1 = ((bf16[8,2,9216]{2,1,0:T(2,128)(2,1)}), bf16[8,2,9216]{2,1,0:T(2,128)(2,1)S(1)}, u32[]{:S(2)}, u32[]{:S(2)}) async-start(bf16[8,2,9216]{2,1,0:T(2,128)(2,1)} %reshape.41), calls=%async_computation.1 | async-start | bytes 589824 | tf_op jit(solution)/shard_map/all_to_all | solution.py:79
  72.3 19.1 %all-to-all-start = ((bf16[2,1,32,4608]{3,0,1,2:T(2,128)(2,1)}), bf16[2,1,32,4608]{3,0,1,2:T(2,128)(2,1)S(1)}, u32[]{:S(2)}, u32[]{:S(2)}) async-start(bf16[2,1,32,4608]{3,0,1,2:T(2,128)(2,1)} %copy.18), calls=%async_computation | async-start | bytes 1179648 | tf_op jit(solution)/shard_map/all_to_all | solution.py:62
